TPU v7x, 256 devices: a whole 4x4x8 slice. The times are simulated.
256 devices in a mesh: row: 8 (over y, core), col: 32 (over x, z).
Axes of the slice: x: 4, y: 4, z: 8, core: 2. Of those that a mesh axis runs over, the one named last changes fastest.
Arguments:
- adjacency: int32 [27136, 27136], P('row', 'col'), may hold values from 0 to 3
- degree: int32 [27136], replicated, may hold values from 64 to 511
- cotangent: bfloat16 [27136, 512], P(('row', 'col')), may hold values from -6 to 6
- features: bfloat16 [27136, 512], P('col'), may hold values from -0.029907227 to 0.029907227
- weight: bfloat16 [512, 512], replicated, may hold values from -0.25 to 0.25
Outputs:
- grad_input: bfloat16 [27136, 512], P('col', 'row')
- grad_weight: float32 [512, 512], P('col', 'row')
All inputs are finite; a program needn't handle non-finite values.
Results may differ from a plain program's by a relative error of at most 0.0058.
Values may be sent and summed in bfloat16 or wider, within the bound.
No kernel may reach another device: no remote copies, remote signals or barrier semaphores. Data moves between devices by JAX's collectives and lax.ppermute only.
A program may use at most 128 MiB of HBM per device.

v0:
```python
import jax
import jax.numpy as jnp
from jax import lax
from jax.sharding import Mesh
from jax.sharding import PartitionSpec as P

COL = ("col_0", "col_1")
ROW_COL = ("row", "col_0", "col_1")


def laid_out(blocks, dim):
    lengths = list(blocks.shape[1:])
    lengths[dim] *= blocks.shape[0]
    return jnp.moveaxis(blocks, 0, dim).reshape(lengths)


def gather_in_order(value, axes, turns):
    blocks = value[None]
    for k in turns:
        blocks = lax.all_gather(blocks, axes[k], axis=0, tiled=True)
    current = [lax.axis_size(axes[k]) for k in reversed(turns)]
    blocks = blocks.reshape(*current, *value.shape)
    turned = sorted(range(len(turns)), key=lambda place: turns[len(turns) - 1 - place])
    return blocks.transpose(*turned, *range(len(turns), blocks.ndim)).reshape(-1, *value.shape)


def gather_axes(value, axes, turns, dim):
    return laid_out(gather_in_order(value, axes, turns), dim)


def split_up(value, dim, length):
    lengths = value.shape
    blocks = value.reshape(*lengths[:dim], length, lengths[dim] // length, *lengths[dim + 1 :])
    return jnp.moveaxis(blocks, dim, 0)


def summed_on_arrival(value, axis, dim):
    blocks = split_up(value, dim, lax.axis_size(axis))
    arrived = lax.all_to_all(blocks, axis, split_axis=0, concat_axis=0, tiled=True)
    return arrived.sum(axis=0)


def copy_for_each(value, axis):
    copies = jnp.broadcast_to(value, (lax.axis_size(axis), *value.shape))
    return lax.all_to_all(copies, axis, split_axis=0, concat_axis=0, tiled=True)


def collect(value, axis, dim):
    return laid_out(copy_for_each(value, axis), dim)


def per_device(adjacency, degree, cotangent, features, weight):
    rows_here, cols_here = adjacency.shape
    row_index = lax.axis_index("row")
    col_index = lax.axis_index(COL)
    inv_root = lax.rsqrt(degree.astype(jnp.float32))
    row_scale = lax.dynamic_slice_in_dim(inv_root, row_index * rows_here, rows_here, 0)
    col_scale = lax.dynamic_slice_in_dim(inv_root, col_index * cols_here, cols_here, 0)
    tile = adjacency.astype(jnp.bfloat16)
    width = weight.shape[0]
    scaled = (
        gather_axes(cotangent, COL, (0, 1), 0).astype(jnp.float32) * row_scale[:, None]
    ).astype(jnp.bfloat16)
    partial_sum = lax.dot_general(
        tile, scaled, (((0,), (0,)), ((), ())), preferred_element_type=jnp.float32
    )
    share = width // lax.axis_size("row")
    weight_rows = lax.dynamic_slice_in_dim(weight, row_index * share, share, 0)
    pieces = summed_on_arrival(partial_sum, "row", 1)
    z_columns = (pieces * col_scale[:, None]).astype(jnp.bfloat16)
    grad_z = collect(z_columns, "row", 1)
    grad_input = lax.dot_general(
        grad_z, weight_rows, (((1,), (1,)), ((), ())), preferred_element_type=jnp.float32
    )
    weight_term = lax.dot_general(
        features, z_columns, (((0,), (0,)), ((), ())), preferred_element_type=jnp.float32
    )
    grad_weight = summed_on_arrival(weight_term, COL, 0)
    return (grad_input.astype(jnp.bfloat16), grad_weight)


def solution(mesh):
    torus = Mesh(mesh.devices.reshape(mesh.shape["row"], 4, 8), ("row", "col_0", "col_1"))
    placed = (P("row", COL), P(), P(ROW_COL, None), P(COL, None), P())
    return jax.shard_map(
        per_device,
        mesh=torus,
        in_specs=placed,
        out_specs=(P(COL, "row"), P(COL, "row")),
        check_vma=False,
    )
```

profile of v0, /device:TPU:1, one launch (start us, length us, event | category | flops | bytes accessed | tf_op | source)
XLA Modules:
  0.0 172.6 jit_solution(2381927909333478503)
XLA Ops:
  7.2 0.0 copy-start
  7.2 0.0 all-gather.4.cloned.1.call-start
  7.2 13.1 %all-gather.1 = bf16[4,106,512]{2,1,0:T(8,128)(2,1)} all-gather(bf16[1,106,512]{2,1,0:T(8,128)(2,1)} %bitcast.23), channel_id=2, replica_groups=mesh['row'=8,'col_0'=4,'col_1'=8] {'col_0'}, dimensions={0}, use_global_device_ids=true | all-gather | bytes 542720 | tf_op jit(solution)/shard_map/all_gather | solution.py:20
  20.3 0.0 all-gather.4.cloned.1.call-update
  20.4 0.9 convert_rsqrt_fusion
  21.3 0.1 dynamic_slice.9
  21.4 53.0 %all-gather.4.cloned.1.call-done = bf16[32,106,512]{2,1,0:T(8,128)(2,1)} async-done(((bf16[4,106,512]{2,1,0:T(8,128)(2,1)}), bf16[32,106,512]{2,1,0:T(8,128)(2,1)}) %all-gather.4.cloned.1.call-update) | async-done | bytes 3473424 | tf_op jit(solution)/shard_map/all_gather | solution.py:20
  74.3 6.1 %copy_bitcast_fusion = f32[4,8,106,512]{3,2,1,0:T(8,128)} fusion(bf16[8,4,106,512]{3,2,1,0:T(8,128)(2,1)} %bitcast.21), kind=kLoop, calls=%fused_computation | loop fusion | flops 1736704 | bytes 10420224 | tf_op jit(solution)/shard_map/convert_element_type | solution.py:62
  80.4 6.6 %reshape.23 = f32[3392,512]{1,0:T(8,128)} reshape(f32[4,8,106,512]{3,2,1,0:T(8,128)} %copy_bitcast_fusion) | data formatting | bytes 13893632 | tf_op jit(solution)/shard_map/convert_element_type | solution.py:62
  87.0 9.7 %fusion.3 = f32[848,512]{1,0:T(8,128)S(1)} fusion(f32[3392,512]{1,0:T(8,128)} %reshape.23, f32[3392]{0:T(1024)S(1)} %dynamic_slice.9, s32[3392,848]{0,1:T(8,128)} %param.5), kind=kOutput, calls=%fused_computation.5 | convolution fusion | flops 2951799808 | bytes 20202752 | tf_op jit(solution)/shard_map/dot_general | solution.py:64
  96.7 1.7 copy.11
  98.4 5.1 %all-to-all-start = ((f32[8,848,64]{1,2,0:T(8,128)}), f32[8,848,64]{1,2,0:T(8,128)S(1)}, u32[]{:S(2)}, u32[]{:S(2)}) async-start(f32[8,848,64]{1,2,0:T(8,128)} %bitcast.19), calls=%async_computation | async-start | bytes 3670016 | tf_op jit(solution)/shard_map/all_to_all | solution.py:39
  103.5 0.1 dynamic_slice.10
  103.6 23.3 %all-to-all-done = f32[8,848,64]{1,2,0:T(8,128)S(1)} async-done(((f32[8,848,64]{1,2,0:T(8,128)}), f32[8,848,64]{1,2,0:T(8,128)S(1)}, u32[]{:S(2)}, u32[]{:S(2)}) %all-to-all-start) | async-done | bytes 1736736 | tf_op jit(solution)/shard_map/all_to_all | solution.py:39
  126.9 0.1 reduce_sum.18
  127.0 0.0 copy-done
  127.0 0.3 convolution_bitcast_fusion
  127.3 0.1 copy.12
  127.5 0.2 reshape.29
  127.7 15.8 %all_to_all.15 = f32[32,1,1024]{2,1,0:T(1,128)S(1)} all-to-all(f32[32,1,1024]{2,1,0:T(1,128)S(1)} %reshape.29), channel_id=1, replica_groups=mesh['row'=8,'col_0'=4,'col_1'=8] {'col_0','col_1'}, dimensions={0} | all-to-all | bytes 262144 | tf_op jit(solution)/shard_map/all_to_all | solution.py:39
  143.5 1.0 broadcast_in_dim.9
  144.5 5.8 %all-to-all-start.1 = ((bf16[8,848,64]{1,2,0:T(8,128)(2,1)}), bf16[8,848,64]{1,2,0:T(8,128)(2,1)S(1)}, u32[]{:S(2)}, u32[]{:S(2)}) async-start(bf16[8,848,64]{1,2,0:T(8,128)(2,1)} %broadcast_in_dim.9), calls=%async_computation.1 | async-start | bytes 1835008 | tf_op jit(solution)/shard_map/all_to_all | solution.py:45
  150.3 0.5 broadcast.2
  150.9 0.9 reduce
  151.8 0.1 reshape.30
  151.9 0.6 reduce_sum.19
  152.6 11.4 %all-to-all-done.1 = bf16[8,848,64]{1,2,0:T(8,128)(2,1)S(1)} async-done(((bf16[8,848,64]{1,2,0:T(8,128)(2,1)}), bf16[8,848,64]{1,2,0:T(8,128)(2,1)S(1)}, u32[]{:S(2)}, u32[]{:S(2)}) %all-to-all-start.1) | async-done | bytes 868384 | tf_op jit(solution)/shard_map/all_to_all | solution.py:45
  163.9 1.8 %convolution_convert_fusion = bf16[848,64]{0,1:T(8,128)(2,1)} fusion(bf16[848,512]{0,1:T(8,128)(2,1)S(1)} %bitcast.20, bf16[512,512]{1,0:T(8,128)(2,1)} %param.9, s32[]{:T(128)S(6)} %select_n.11), kind=kOutput, calls=%fused_computation.6 | convolution fusion | flops 55628800 | bytes 1042436 | tf_op jit(solution)/shard_map/dot_general | solution.py:72
  (1 shorter events, 0.0 us)
Async XLA Ops:
  7.2 119.9 %copy-start = (bf16[848,512]{1,0:T(8,128)(2,1)S(1)}, bf16[848,512]{1,0:T(8,128)(2,1)}, u32[]{:S(2)}) copy-start(bf16[848,512]{1,0:T(8,128)(2,1)} %param.8) | copy-start | bytes 2605060
  7.2 67.2 %all-gather.4.cloned.1.call-start = ((), (), s32[]{:S(2)}) async-start(), calls=%async_computation.3 | async-start | bytes 4128768 | tf_op jit(solution)/shard_map/all_gather | solution.py:20
  98.4 28.5 %all-to-all-start = ((f32[8,848,64]{1,2,0:T(8,128)}), f32[8,848,64]{1,2,0:T(8,128)S(1)}, u32[]{:S(2)}, u32[]{:S(2)}) async-start(f32[8,848,64]{1,2,0:T(8,128)} %bitcast.19), calls=%async_computation | async-start | bytes 3670016 | tf_op jit(solution)/shard_map/all_to_all | solution.py:39
  144.5 19.4 %all-to-all-start.1 = ((bf16[8,848,64]{1,2,0:T(8,128)(2,1)}), bf16[8,848,64]{1,2,0:T(8,128)(2,1)S(1)}, u32[]{:S(2)}, u32[]{:S(2)}) async-start(bf16[8,848,64]{1,2,0:T(8,128)(2,1)} %broadcast_in_dim.9), calls=%async_computation.1 | async-start | bytes 1835008 | tf_op jit(solution)/shard_map/all_to_all | solution.py:45
Sparse Core Ops, SparseCore 0:
  20.5 53.8 all-gather.3
where the time goes:
time: 173 us
  waiting for transfers between devices  87.7 us (51%)
  blocking collectives  28.9 us (17%)
  between operations  14.1 us (8%)
  matrix products  11.7 us (7%)
  starting transfers between devices  11 us (6%)
  local copies, waits for them, and re-layouts  10.5 us (6%)
  other arithmetic  8.69 us (5%)
    all_gather x1, waiting for transfers between devices, gather_in_order(): blocks = lax.all_gather(blocks, axes[k], axis=0, tiled=True)  53 us
    all_to_all x1, waiting for transfers between devices, summed_on_arrival(): lax.all_to_all(blocks, axis, split_axis=0, concat_axis=0, tiled=True)  23.3 us
    all_to_all x1, blocking collectives, summed_on_arrival(): lax.all_to_all(blocks, axis, split_axis=0, concat_axis=0, tiled=True)  15.8 us
    all_gather x1, blocking collectives, gather_in_order(): blocks = lax.all_gather(blocks, axes[k], axis=0, tiled=True)  13.1 us
    all_to_all x1, waiting for transfers between devices, copy_for_each(): return lax.all_to_all(copies, axis, split_axis=0, concat_axis=0, tiled=True)  11.4 us
    dot_general x1, matrix products, per_device(): lax.dot_general(tile, scaled, (((0,), (0,)), ((), ())), preferred_element...  9.67 us
    convert_element_type x1, local copies, waits for them, and re-layouts, per_device(): gather_axes(cotangent, COL, (0, 1), 0).astype(jnp.float32)  6.6 us
    convert_element_type x1, other arithmetic, per_device(): gather_axes(cotangent, COL, (0, 1), 0).astype(jnp.float32)  6.06 us
  transfers between devices with their start and end apart: 3, of which 3 were waited for; matrix products, arithmetic and copies ran while one was open for 2% of the time, Pallas kernels for 0%

commit v1 on v0

--- a/solution.py
+++ b/solution.py
@@ -17,7 +17,8 @@
 def gather_in_order(value, axes, turns):
     blocks = value[None]
     for k in turns:
-        blocks = lax.all_gather(blocks, axes[k], axis=0, tiled=True)
+        sent = jnp.stack([blocks] * lax.axis_size(axes[k]))
+        blocks = jnp.concatenate(lax.all_to_all(sent, axes[k], 0, 0), axis=0)
     current = [lax.axis_size(axes[k]) for k in reversed(turns)]
     blocks = blocks.reshape(*current, *value.shape)
     turned = sorted(range(len(turns)), key=lambda place: turns[len(turns) - 1 - place])

time: 173 us -> 197 us (1.14)
  waiting for transfers between devices: 87.7 us -> 116 us
  between operations: 14.1 us -> 0.73 us
  local copies, waits for them, and re-layouts: 10.5 us -> 19.6 us
  starting transfers between devices: 11 us -> 18.7 us
  blocking collectives: 28.9 us -> 24.4 us
  other arithmetic: 8.69 us -> 5.05 us
    all_to_all x0 -> x1, waiting for transfers between devices: none -> 81.2 us  [gather_in_order(): blocks = jnp.concatenate(lax.all_to_all(sent, axes[k], 0, 0), axis=0)]
    all_gather x1 -> x0, waiting for transfers between devices: 53 us -> none  [gather_in_order(): blocks = lax.all_gather(blocks, axes[k], axis=0, tiled=True)]
    all_gather x1 -> x0, blocking collectives: 13.1 us -> none  [gather_in_order(): blocks = lax.all_gather(blocks, axes[k], axis=0, tiled=True)]
    all_to_all x0 -> x1, blocking collectives: none -> 12.3 us  [gather_in_order(): blocks = jnp.concatenate(lax.all_to_all(sent, axes[k], 0, 0), axis=0)]
    all_to_all x0 -> x1, starting transfers between devices: none -> 8.19 us  [gather_in_order(): blocks = jnp.concatenate(lax.all_to_all(sent, axes[k], 0, 0), axis=0)]
    convert_element_type x1 -> x2, local copies, waits for them, and re-layouts: 6.6 us -> 11.7 us  [per_device(): gather_axes(cotangent, COL, (0, 1), 0).astype(jnp.float32)]
    another operation x0 -> x3, local copies, waits for them, and re-layouts: none -> 4.06 us  [gather_in_order(): sent = jnp.stack([blocks] * lax.axis_size(axes[k]))]
    all_to_all x1, blocking collectives: 15.8 us -> 12.1 us  [summed_on_arrival(): lax.all_to_all(blocks, axis, split_axis=0, concat_axis=0, tiled=True)]
  transfers between devices with their start and end apart: 3 -> 3, of which waited for: 3 -> 3; matrix products, arithmetic and copies ran while one was open for 2% -> 1% of each run, Pallas kernels for 0% -> 0%
where the time goes in v1:
time: 197 us; the launch traced here: 196 us
  waiting for transfers between devices  116 us (59%)
  blocking collectives  24.4 us (12%)
  local copies, waits for them, and re-layouts  19.6 us (10%)
  starting transfers between devices  18.7 us (9%)
  matrix products  11.7 us (6%)
  other arithmetic  5.05 us (3%)
    all_to_all x1, waiting for transfers between devices, gather_in_order(): blocks = jnp.concatenate(lax.all_to_all(sent, axes[k], 0, 0), axis=0)  81.2 us
    all_to_all x1, waiting for transfers between devices, summed_on_arrival(): lax.all_to_all(blocks, axis, split_axis=0, concat_axis=0, tiled=True)  23.3 us
    all_to_all x1, blocking collectives, gather_in_order(): blocks = jnp.concatenate(lax.all_to_all(sent, axes[k], 0, 0), axis=0)  12.3 us
    all_to_all x1, blocking collectives, summed_on_arrival(): lax.all_to_all(blocks, axis, split_axis=0, concat_axis=0, tiled=True)  12.1 us
    convert_element_type x2, local copies, waits for them, and re-layouts, per_device(): gather_axes(cotangent, COL, (0, 1), 0).astype(jnp.float32)  11.7 us
    all_to_all x1, waiting for transfers between devices, copy_for_each(): return lax.all_to_all(copies, axis, split_axis=0, concat_axis=0, tiled=True)  11.4 us
    dot_general x1, matrix products, per_device(): lax.dot_general(tile, scaled, (((0,), (0,)), ((), ())), preferred_element...  9.68 us
    all_to_all x1, starting transfers between devices, gather_in_order(): blocks = jnp.concatenate(lax.all_to_all(sent, axes[k], 0, 0), axis=0)  8.19 us
  transfers between devices with their start and end apart: 3, of which 3 were waited for; matrix products, arithmetic and copies ran while one was open for 1% of the time, Pallas kernels for 0%

profile of v1, /device:TPU:1, one launch (start us, length us, event | category | flops | bytes accessed | tf_op | source)
XLA Modules:
  0.0 196.1 jit_solution(8359455302871700676)
XLA Ops:
  0.6 0.0 copy-start
  0.6 0.0 copy-start.1
  0.7 1.0 stack.6
  1.7 12.3 %all_to_all.25 = bf16[4,1,106,512]{3,2,1,0:T(8,128)(2,1)S(1)} all-to-all(bf16[4,1,106,512]{3,2,1,0:T(8,128)(2,1)S(1)} %stack.6), channel_id=1, replica_groups=mesh['row'=8,'col_0'=4,'col_1'=8] {'col_0'}, dimensions={0} | all-to-all | bytes 868352 | tf_op jit(solution)/shard_map/all_to_all | solution.py:21
  13.9 0.3 copy.9
  14.3 2.7 %stack.7 = bf16[8,4,106,512]{3,1,2,0:T(4,128)(2,1)} broadcast(bf16[4,106,512]{2,0,1:T(4,128)(2,1)S(1)} %copy.9), dimensions={1,2,3} | broadcast | bytes 3907584 | tf_op jit(solution)/shard_map/stack | solution.py:20
  17.0 8.2 %all-to-all-start.1 = ((bf16[8,4,106,512]{3,1,2,0:T(4,128)(2,1)}), bf16[8,4,106,512]{3,1,2,0:T(4,128)(2,1)}, u32[]{:S(2)}, u32[]{:S(2)}) async-start(bf16[8,4,106,512]{3,1,2,0:T(4,128)(2,1)} %stack.7), calls=%async_computation.1 | async-start | bytes 6946816 | tf_op jit(solution)/shard_map/all_to_all | solution.py:21
  25.2 0.0 copy-done.1
  25.2 0.1 dynamic_slice.9
  25.3 81.2 %all-to-all-done.1 = bf16[8,4,106,512]{3,1,2,0:T(4,128)(2,1)} async-done(((bf16[8,4,106,512]{3,1,2,0:T(4,128)(2,1)}), bf16[8,4,106,512]{3,1,2,0:T(4,128)(2,1)}, u32[]{:S(2)}, u32[]{:S(2)}) %all-to-all-start.1) | async-done | bytes 3473440 | tf_op jit(solution)/shard_map/all_to_all | solution.py:21
  106.5 3.3 %convert_bitcast_fusion = f32[4,8,106,512]{3,0,2,1:T(4,128)S(1)} fusion(bf16[8,4,106,512]{3,1,2,0:T(4,128)(2,1)} %all-to-all-done.1), kind=kLoop, calls=%fused_computation | loop fusion | flops 1736704 | bytes 10420224 | tf_op jit(solution)/shard_map/convert_element_type | solution.py:63
  109.8 5.1 %copy.10 = f32[4,8,106,512]{3,2,1,0:T(8,128)} copy(f32[4,8,106,512]{3,0,2,1:T(4,128)S(1)} %convert_bitcast_fusion) | data formatting | bytes 13893632 | tf_op jit(solution)/shard_map/convert_element_type | solution.py:63
  114.9 6.6 %reshape.24 = f32[3392,512]{1,0:T(8,128)} reshape(f32[4,8,106,512]{3,2,1,0:T(8,128)} %copy.10) | data formatting | bytes 13893632 | tf_op jit(solution)/shard_map/convert_element_type | solution.py:63
  121.5 9.7 %fusion.3 = f32[848,512]{1,0:T(8,128)S(1)} fusion(f32[3392,512]{1,0:T(8,128)} %reshape.24, f32[3392]{0:T(1024)S(1)} %dynamic_slice.9, s32[3392,848]{0,1:T(8,128)} %param.5), kind=kOutput, calls=%fused_computation.5 | convolution fusion | flops 2951799808 | bytes 20202752 | tf_op jit(solution)/shard_map/dot_general | solution.py:65
  131.2 1.7 copy.11
  132.9 4.9 %all-to-all-start.2 = ((f32[8,848,64]{1,2,0:T(8,128)}), f32[8,848,64]{1,2,0:T(8,128)S(1)}, u32[]{:S(2)}, u32[]{:S(2)}) async-start(f32[8,848,64]{1,2,0:T(8,128)} %bitcast.17), calls=%async_computation.2 | async-start | bytes 3670016 | tf_op jit(solution)/shard_map/all_to_all | solution.py:40
  137.9 0.1 dynamic_slice.10
  138.0 23.3 %all-to-all-done.2 = f32[8,848,64]{1,2,0:T(8,128)S(1)} async-done(((f32[8,848,64]{1,2,0:T(8,128)}), f32[8,848,64]{1,2,0:T(8,128)S(1)}, u32[]{:S(2)}, u32[]{:S(2)}) %all-to-all-start.2) | async-done | bytes 1736736 | tf_op jit(solution)/shard_map/all_to_all | solution.py:40
  161.3 0.1 reduce_sum.18
  161.4 0.0 copy-done
  161.4 0.3 convolution_bitcast_fusion
  161.7 0.1 copy.12
  161.8 0.2 reshape.25
  162.0 12.1 %all_to_all.26 = f32[32,1,1024]{2,1,0:T(1,128)S(1)} all-to-all(f32[32,1,1024]{2,1,0:T(1,128)S(1)} %reshape.25), channel_id=1, replica_groups=mesh['row'=8,'col_0'=4,'col_1'=8] {'col_0','col_1'}, dimensions={0} | all-to-all | bytes 262144 | tf_op jit(solution)/shard_map/all_to_all | solution.py:40
  174.2 1.0 broadcast_in_dim.2
  175.2 5.6 %all-to-all-start.3 = ((bf16[8,848,64]{1,2,0:T(8,128)(2,1)}), bf16[8,848,64]{1,2,0:T(8,128)(2,1)S(1)}, u32[]{:S(2)}, u32[]{:S(2)}) async-start(bf16[8,848,64]{1,2,0:T(8,128)(2,1)} %broadcast_in_dim.2), calls=%async_computation.3 | async-start | bytes 1835008 | tf_op jit(solution)/shard_map/all_to_all | solution.py:46
  180.8 0.5 broadcast.5
  181.3 0.9 reduce
  182.2 0.1 reshape.26
  182.3 0.6 reduce_sum.19
  183.0 11.4 %all-to-all-done.3 = bf16[8,848,64]{1,2,0:T(8,128)(2,1)S(1)} async-done(((bf16[8,848,64]{1,2,0:T(8,128)(2,1)}), bf16[8,848,64]{1,2,0:T(8,128)(2,1)S(1)}, u32[]{:S(2)}, u32[]{:S(2)}) %all-to-all-start.3) | async-done | bytes 868384 | tf_op jit(solution)/shard_map/all_to_all | solution.py:46
  194.4 1.8 convolution_convert_fusion
  (2 shorter events, 0.0 us)
Async XLA Ops:
  0.6 160.8 %copy-start = (bf16[848,512]{1,0:T(8,128)(2,1)S(1)}, bf16[848,512]{1,0:T(8,128)(2,1)}, u32[]{:S(2)}) copy-start(bf16[848,512]{1,0:T(8,128)(2,1)} %param.8) | copy-start | bytes 2605060
  0.6 24.5 %copy-start.1 = (s32[27136]{0:T(1024)S(1)}, s32[27136]{0:T(1024)}, u32[]{:S(2)}) copy-start(s32[27136]{0:T(1024)} %param.6) | copy-start | bytes 325636
  17.0 89.5 %all-to-all-start.1 = ((bf16[8,4,106,512]{3,1,2,0:T(4,128)(2,1)}), bf16[8,4,106,512]{3,1,2,0:T(4,128)(2,1)}, u32[]{:S(2)}, u32[]{:S(2)}) async-start(bf16[8,4,106,512]{3,1,2,0:T(4,128)(2,1)} %stack.7), calls=%async_computation.1 | async-start | bytes 6946816 | tf_op jit(solution)/shard_map/all_to_all | solution.py:21
  132.9 28.3 %all-to-all-start.2 = ((f32[8,848,64]{1,2,0:T(8,128)}), f32[8,848,64]{1,2,0:T(8,128)S(1)}, u32[]{:S(2)}, u32[]{:S(2)}) async-start(f32[8,848,64]{1,2,0:T(8,128)} %bitcast.17), calls=%async_computation.2 | async-start | bytes 3670016 | tf_op jit(solution)/shard_map/all_to_all | solution.py:40
  175.2 19.2 %all-to-all-start.3 = ((bf16[8,848,64]{1,2,0:T(8,128)(2,1)}), bf16[8,848,64]{1,2,0:T(8,128)(2,1)S(1)}, u32[]{:S(2)}, u32[]{:S(2)}) async-start(bf16[8,848,64]{1,2,0:T(8,128)(2,1)} %broadcast_in_dim.2), calls=%async_computation.3 | async-start | bytes 1835008 | tf_op jit(solution)/shard_map/all_to_all | solution.py:46
